TPU v7x, 32 devices: a whole 2x2x4 slice. The times are simulated.
32 devices in a mesh: tm: 4 (over x, core), anta: 4 (over z), antb: 2 (over y).
Axes of the slice: x: 2, y: 2, z: 4, core: 2. Of those that a mesh axis runs over, the one named last changes fastest.
Arguments:
- samples: bfloat16 [2, 512, 6144], P('antb', 'anta', 'tm'), may hold values from -6 to 6
Outputs:
- correlation: float32 [256, 2, 512, 2, 512], P('tm', None, 'anta', 'antb')
All inputs are finite; a program needn't handle non-finite values.
Results may differ from a plain program's by a relative error of at most 0.0003.
Values may be sent and summed in bfloat16 or wider, within the bound.
A program may use at most 128 MiB of HBM per device.

v0:
```python
import math

import jax
import jax.numpy as jnp
from jax import lax
from jax.sharding import PartitionSpec as P

ANTENNA_COUNT = 512
POLARISATION_NUM = 2
LAG_TOTAL = 256


def lag_terms(row_padded, columns, lag_start, lag_count, window_len):
    group_len = math.gcd(lag_count, 8)
    flat_cols = columns.reshape(columns.shape[1], columns.shape[2])

    def one_group(group_index):
        first_lag = lag_start + group_index * group_len
        pieces = [
            lax.dynamic_slice_in_dim(row_padded, LAG_TOTAL - first_lag - step_index, window_len, 1)
            for step_index in range(group_len)
        ]
        stacked = jnp.stack(pieces, 0)
        return jnp.einsum("kit,jt->kij", stacked, flat_cols, preferred_element_type=jnp.float32)

    grouped = lax.map(one_group, jnp.arange(lag_count // group_len, dtype=jnp.int32))
    return grouped.reshape(lag_count, row_padded.shape[0], flat_cols.shape[0])


def collect_rows(own_window):
    return lax.all_gather(own_window, "antb", axis=0, tiled=True)


def per_device(samples):
    antenna_total = samples.shape[1]
    block_len = samples.shape[2]
    tm_size = lax.axis_size("tm")
    lag_portion = LAG_TOTAL // tm_size
    full_length = block_len * tm_size
    factor = 1.0 / math.sqrt(full_length)
    lag_start = lax.axis_index("tm") * lag_portion
    col_tiles = lax.all_gather(samples, "anta", axis=1, tiled=True)
    columns = lax.all_gather(col_tiles, "tm", axis=2, tiled=True)
    own_rows = lax.dynamic_slice_in_dim(
        columns, lax.axis_index("anta") * antenna_total, antenna_total, 1
    )
    row_samples = collect_rows(own_rows)
    row_padded = jnp.pad(
        row_samples.reshape(POLARISATION_NUM * antenna_total, full_length), ((0, 0), (LAG_TOTAL, 0))
    )
    lag_group_block = lag_terms(row_padded, columns, lag_start, lag_portion, full_length)
    accumulated_sum = lag_group_block.reshape(
        lag_portion, POLARISATION_NUM, antenna_total, 1, ANTENNA_COUNT
    )
    return accumulated_sum * factor


def solution(mesh):
    return jax.shard_map(
        per_device,
        mesh=mesh,
        in_specs=(P("antb", "anta", "tm"),),
        out_specs=P("tm", None, "anta", "antb", None),
        check_vma=False,
    )
```

profile of v0, /device:TPU:0, one launch (start us, length us, event | category | flops | bytes accessed | tf_op | source)
XLA Modules:
  0.0 584.9 jit_solution(11511170079034413192)
XLA Ops:
  7.3 41.4 %all-gather.4.cloned.1.call-done = bf16[1,512,1536]{2,1,0:T(8,128)(2,1)} async-done(((bf16[1,128,1536]{2,1,0:T(8,128)(2,1)}), bf16[1,512,1536]{2,1,0:T(8,128)(2,1)}) %all-gather.4.cloned.1.call-update) | async-done | bytes 1572880 | tf_op jit(solution)/shard_map/all_gather | solution.py:42
  48.8 46.7 %all-gather.6.cloned.1.call-done = bf16[1,512,6144]{2,1,0:T(8,128)(2,1)} async-done(((bf16[1,512,1536]{2,1,0:T(8,128)(2,1)}), bf16[1,512,6144]{2,1,0:T(8,128)(2,1)}) %all-gather.6.cloned.1.call-update) | async-done | bytes 6291472 | tf_op jit(solution)/shard_map/all_gather | solution.py:43
  98.2 45.1 %all-gather.8.cloned.1.call-done = bf16[2,128,6144]{2,1,0:T(8,128)(2,1)} async-done(((bf16[1,128,6144]{2,1,0:T(8,128)(2,1)}), bf16[2,128,6144]{2,1,0:T(8,128)(2,1)}) %all-gather.8.cloned.1.call-update) | async-done | bytes 3145744 | tf_op jit(solution)/shard_map/all_gather | solution.py:31
  145.4 360.6 %while.14 = (s32[]{:T(128)}, f32[8,8,256,512]{3,2,1,0:T(8,128)}, s32[8]{0:T(128)S(1)}, s32[]{:T(128)}, bf16[256,6400]{1,0:T(8,128)(2,1)S(1)}, /*index=5*/bf16[51...) while((s32[]{:T(128)}, f32[8,8,256,512]{3,2,1,0:T(8,128)}, ...), condition=%wide.region_1.2_spmd, body=%wide.region_0.1_spmd.sunk | while | flops 12884901888 | bytes 85984392 | solution.py:26
  149.5 2.9 bitcast_dynamic-update-slice_fusion.19
  152.4 2.9 bitcast_dynamic-update-slice_fusion.20
  169.4 21.0 %bitcast_dynamic-update-slice_fusion.26 = f32[8,8,256,512]{3,2,1,0:T(8,128)} fusion(f32[8,8,256,512]{3,2,1,0:T(8,128)} %get-tuple-element.216, s32[]{:T(128)} %get-tuple-element.215, bf16[8,256,6144]{2,1,0:T(8,128)(2,1)} %bitcast_dynamic-update-slice_fusion.25, bf16[512,6144]{1,0:T(8,128)(2,1)} %get-tuple-element.245), kind=kOutput, calls=%fused_computation.2.clone.1 | convolution fusion | flops 12884901888 | bytes 35652096 | tf_op jit(solution)/shard_map/while/body/eval_jaxpr/kit,jt->kij/dot_general | solution.py:24
  194.6 2.9 bitcast_dynamic-update-slice_fusion.19
  197.5 2.9 bitcast_dynamic-update-slice_fusion.20
  214.5 21.1 %bitcast_dynamic-update-slice_fusion.26 = f32[8,8,256,512]{3,2,1,0:T(8,128)} fusion(f32[8,8,256,512]{3,2,1,0:T(8,128)} %get-tuple-element.216, s32[]{:T(128)} %get-tuple-element.215, bf16[8,256,6144]{2,1,0:T(8,128)(2,1)} %bitcast_dynamic-update-slice_fusion.25, bf16[512,6144]{1,0:T(8,128)(2,1)} %get-tuple-element.245), kind=kOutput, calls=%fused_computation.2.clone.1 | convolution fusion | flops 12884901888 | bytes 35652096 | tf_op jit(solution)/shard_map/while/body/eval_jaxpr/kit,jt->kij/dot_general | solution.py:24
  236.8 2.8 bitcast_dynamic-update-slice_fusion.18
  239.7 2.9 bitcast_dynamic-update-slice_fusion.19
  242.6 2.9 bitcast_dynamic-update-slice_fusion.20
  259.6 21.1 %bitcast_dynamic-update-slice_fusion.26 = f32[8,8,256,512]{3,2,1,0:T(8,128)} fusion(f32[8,8,256,512]{3,2,1,0:T(8,128)} %get-tuple-element.216, s32[]{:T(128)} %get-tuple-element.215, bf16[8,256,6144]{2,1,0:T(8,128)(2,1)} %bitcast_dynamic-update-slice_fusion.25, bf16[512,6144]{1,0:T(8,128)(2,1)} %get-tuple-element.245), kind=kOutput, calls=%fused_computation.2.clone.1 | convolution fusion | flops 12884901888 | bytes 35652096 | tf_op jit(solution)/shard_map/while/body/eval_jaxpr/kit,jt->kij/dot_general | solution.py:24
  281.9 2.8 bitcast_dynamic-update-slice_fusion.18
  284.8 2.9 bitcast_dynamic-update-slice_fusion.19
  287.6 2.9 bitcast_dynamic-update-slice_fusion.20
  304.7 21.1 %bitcast_dynamic-update-slice_fusion.26 = f32[8,8,256,512]{3,2,1,0:T(8,128)} fusion(f32[8,8,256,512]{3,2,1,0:T(8,128)} %get-tuple-element.216, s32[]{:T(128)} %get-tuple-element.215, bf16[8,256,6144]{2,1,0:T(8,128)(2,1)} %bitcast_dynamic-update-slice_fusion.25, bf16[512,6144]{1,0:T(8,128)(2,1)} %get-tuple-element.245), kind=kOutput, calls=%fused_computation.2.clone.1 | convolution fusion | flops 12884901888 | bytes 35652096 | tf_op jit(solution)/shard_map/while/body/eval_jaxpr/kit,jt->kij/dot_general | solution.py:24
  329.8 2.9 bitcast_dynamic-update-slice_fusion.19
  332.7 2.9 bitcast_dynamic-update-slice_fusion.20
  349.7 21.1 %bitcast_dynamic-update-slice_fusion.26 = f32[8,8,256,512]{3,2,1,0:T(8,128)} fusion(f32[8,8,256,512]{3,2,1,0:T(8,128)} %get-tuple-element.216, s32[]{:T(128)} %get-tuple-element.215, bf16[8,256,6144]{2,1,0:T(8,128)(2,1)} %bitcast_dynamic-update-slice_fusion.25, bf16[512,6144]{1,0:T(8,128)(2,1)} %get-tuple-element.245), kind=kOutput, calls=%fused_computation.2.clone.1 | convolution fusion | flops 12884901888 | bytes 35652096 | tf_op jit(solution)/shard_map/while/body/eval_jaxpr/kit,jt->kij/dot_general | solution.py:24
  374.9 2.9 bitcast_dynamic-update-slice_fusion.19
  377.8 2.9 bitcast_dynamic-update-slice_fusion.20
  394.8 21.1 %bitcast_dynamic-update-slice_fusion.26 = f32[8,8,256,512]{3,2,1,0:T(8,128)} fusion(f32[8,8,256,512]{3,2,1,0:T(8,128)} %get-tuple-element.216, s32[]{:T(128)} %get-tuple-element.215, bf16[8,256,6144]{2,1,0:T(8,128)(2,1)} %bitcast_dynamic-update-slice_fusion.25, bf16[512,6144]{1,0:T(8,128)(2,1)} %get-tuple-element.245), kind=kOutput, calls=%fused_computation.2.clone.1 | convolution fusion | flops 12884901888 | bytes 35652096 | tf_op jit(solution)/shard_map/while/body/eval_jaxpr/kit,jt->kij/dot_general | solution.py:24
  420.0 2.9 bitcast_dynamic-update-slice_fusion.19
  422.9 2.9 bitcast_dynamic-update-slice_fusion.20
  439.9 21.1 %bitcast_dynamic-update-slice_fusion.26 = f32[8,8,256,512]{3,2,1,0:T(8,128)} fusion(f32[8,8,256,512]{3,2,1,0:T(8,128)} %get-tuple-element.216, s32[]{:T(128)} %get-tuple-element.215, bf16[8,256,6144]{2,1,0:T(8,128)(2,1)} %bitcast_dynamic-update-slice_fusion.25, bf16[512,6144]{1,0:T(8,128)(2,1)} %get-tuple-element.245), kind=kOutput, calls=%fused_computation.2.clone.1 | convolution fusion | flops 12884901888 | bytes 35652096 | tf_op jit(solution)/shard_map/while/body/eval_jaxpr/kit,jt->kij/dot_general | solution.py:24
  465.1 2.9 bitcast_dynamic-update-slice_fusion.19
  467.9 2.9 bitcast_dynamic-update-slice_fusion.20
  485.0 21.1 %bitcast_dynamic-update-slice_fusion.26 = f32[8,8,256,512]{3,2,1,0:T(8,128)} fusion(f32[8,8,256,512]{3,2,1,0:T(8,128)} %get-tuple-element.216, s32[]{:T(128)} %get-tuple-element.215, bf16[8,256,6144]{2,1,0:T(8,128)(2,1)} %bitcast_dynamic-update-slice_fusion.25, bf16[512,6144]{1,0:T(8,128)(2,1)} %get-tuple-element.245), kind=kOutput, calls=%fused_computation.2.clone.1 | convolution fusion | flops 12884901888 | bytes 35652096 | tf_op jit(solution)/shard_map/while/body/eval_jaxpr/kit,jt->kij/dot_general | solution.py:24
  506.0 23.9 %broadcast_multiply_fusion = f32[8,8,256,512]{3,2,1,0:T(8,128)} fusion(f32[8,8,256,512]{3,2,1,0:T(8,128)} %get-tuple-element.140), kind=kLoop, calls=%fused_computation.11 | loop fusion | flops 8388608 | bytes 67108864 | tf_op jit(solution)/shard_map/mul | solution.py:55
  530.0 48.4 %mul.39 = f32[64,2,128,1,512]{4,3,2,1,0:T(1,128)} reshape(f32[8,8,256,512]{3,2,1,0:T(8,128)} %broadcast_multiply_fusion) | data formatting | bytes 67108864 | tf_op jit(solution)/shard_map/mul | solution.py:55
  (64 shorter events, 141.0 us)
Async XLA Ops:
  6.5 42.1 %all-gather.4.cloned.1.call-start = ((), (), s32[]{:S(2)}) async-start(), calls=%async_computation | async-start | bytes 1966080 | tf_op jit(solution)/shard_map/all_gather | solution.py:42
  7.3 88.2 %all-gather.6.cloned.1.call-start = ((), (), s32[]{:S(2)}) async-start(), calls=%async_computation.1 | async-start | bytes 7864320 | tf_op jit(solution)/shard_map/all_gather | solution.py:43
  48.7 94.6 %all-gather.8.cloned.1.call-start = ((), (), s32[]{:S(2)}) async-start(), calls=%async_computation.2 | async-start | bytes 4718592 | tf_op jit(solution)/shard_map/all_gather | solution.py:31
Sparse Core Ops, SparseCore 0:
  8.9 39.7 all-gather.3
  50.2 45.2 all-gather.5
  98.3 44.9 all-gather.7
where the time goes:
time: 586 us; the launch traced here: 585 us
  local copies, waits for them, and re-layouts  240 us (41%)
  matrix products  168 us (29%)
  waiting for transfers between devices  134 us (23%)
  other arithmetic  23.9 us (4%)
  between operations  13.1 us (2%)
    dot_general x8, matrix products, one_group(): jnp.einsum('kit,jt->kij', stacked, flat_cols, preferred_element_type=jnp....  168 us
    while x56, local copies, waits for them, and re-layouts  159 us
    mul x1, local copies, waits for them, and re-layouts, per_device(): return accumulated_sum * factor  48.4 us
    all_gather x1, waiting for transfers between devices, per_device(): columns = lax.all_gather(col_tiles, 'tm', axis=2, tiled=True)  46.7 us
    all_gather x1, waiting for transfers between devices, collect_rows(): return lax.all_gather(own_window, 'antb', axis=0, tiled=True)  45.1 us
    all_gather x1, waiting for transfers between devices, per_device(): col_tiles = lax.all_gather(samples, 'anta', axis=1, tiled=True)  41.4 us
    mul x1, other arithmetic, per_device(): return accumulated_sum * factor  23.9 us
    another operation x8, local copies, waits for them, and re-layouts, one_group(): stacked = jnp.stack(pieces, 0)  22.7 us
  transfers between devices with their start and end apart: 3, of which 3 were waited for; matrix products, arithmetic and copies ran while one was open for 0% of the time, Pallas kernels for 0%

commit v1 on v0

v1 whole, which is shorter than its diff:
```python
import functools
import math

import jax
import jax.numpy as jnp
from jax import lax
from jax.experimental import pallas as pl
from jax.experimental.pallas import tpu as pltpu
from jax.sharding import PartitionSpec as P

LAG_TOTAL = 256
LANES = 128


def correlate_kernel(factor, stride, lags, cols_hbm, other_hbm, out_ref, rows, cols, hankel, sems):
    blocks, ring, height = cols_hbm.shape[:3]
    units = blocks * LANES
    window = stride * units
    step = pl.program_id(0)
    lag_start = lax.axis_index("tm") * lags

    def fill(entry):
        back = (lags - 1) + lag_start - entry
        shift = (back + stride - 1) // stride
        residue = shift * stride - back
        tile = rows[:, pl.ds(pl.multiple_of(residue * units, units), units)].astype(jnp.float32)
        rolled = pltpu.roll(tile, shift, 1)
        lane = lax.broadcasted_iota(jnp.int32, rolled.shape, 1)
        rolled = jnp.where(lane >= shift, rolled, 0.0)
        hankel[:, pl.ds(pl.multiple_of(entry * units, units), units)] = rolled.astype(jnp.bfloat16)

    def copies():
        anta, antb = lax.axis_index("anta"), lax.axis_index("antb")
        same = pl.ds(pl.multiple_of(antb * height, height), height)
        cross = pl.ds(pl.multiple_of((1 - antb) * height, height), height)
        for block in range(blocks):
            for r in range(stride):
                src = pl.ds(r * LANES, LANES)
                dst = pl.ds(r * units + block * LANES, LANES)
                yield cols_hbm.at[block, anta, :, src], rows.at[same, dst], sems.at[ring, block, r]
                yield other_hbm.at[block, :, src], rows.at[cross, dst], sems.at[ring + 1, block, r]
        for block in range(blocks):
            for r in range(stride):
                src = pl.ds(r * LANES, LANES)
                dst = pl.ds(r * units + block * LANES, LANES)
                for place in range(ring):
                    there = pl.ds(place * height, height)
                    yield cols_hbm.at[block, place, :, src], cols.at[there, dst], sems.at[place, block, r]

    @pl.when(step == 0)
    def _():
        for src, dst, sem in copies():
            pltpu.make_async_copy(src, dst, sem).start()
        for src, dst, sem in copies():
            pltpu.make_async_copy(src, dst, sem).wait()

        @pl.loop(0, stride)
        def _(index):
            fill(lags - 1 + index)

    @pl.when(step > 0)
    def _():
        fill(lags - 1 - step)

    offset = pl.multiple_of((lags - 1 - step) * units, units)
    lhs = hankel[:, pl.ds(offset, window)]
    res = lax.dot_general(lhs, cols[...], (((1,), (1,)), ((), ())), preferred_element_type=jnp.float32)
    res = res * factor
    pieces = res.shape[1] // LANES
    for piece in range(pieces):
        out_ref[0, pl.ds(piece, res.shape[0], stride=pieces), :] = res[:, piece * LANES:(piece + 1) * LANES]


def correlate(cols, other, lags, factor):
    blocks, ring, height, width = cols.shape
    row_count, col_count = 2 * height, ring * height
    stride = width // LANES
    window = blocks * width
    pieces = col_count // LANES
    return pl.pallas_call(
        functools.partial(correlate_kernel, factor, stride, lags),
        grid=(lags,),
        out_shape=jax.ShapeDtypeStruct((lags, row_count * pieces, LANES), jnp.float32),
        in_specs=[pl.BlockSpec(memory_space=pl.ANY)] * 2,
        out_specs=pl.BlockSpec((1, row_count * pieces, LANES), lambda i: (i, 0, 0)),
        scratch_shapes=[
            pltpu.VMEM((row_count, window), jnp.bfloat16),
            pltpu.VMEM((col_count, window), jnp.bfloat16),
            pltpu.VMEM((row_count, (lags - 1 + stride) * blocks * LANES), jnp.bfloat16),
            pltpu.SemaphoreType.DMA((ring + 2, blocks, stride)),
        ],
        compiler_params=pltpu.CompilerParams(vmem_limit_bytes=60 * 1024 * 1024),
    )(cols, other)


def gather_kernel(own, cols, other, local_sem, ring_send, ring_recv, near_send, near_recv,
                  far_send, far_recv, pol_send, pol_recv):
    tm, anta, antb = (lax.axis_index(name) for name in ("tm", "anta", "antb"))
    blocks, ring = cols.shape[:2]
    height = own.shape[0]
    half = height // 2
    far = lax.rem(tm + blocks // 2, blocks)
    near = tm + 1 - 2 * lax.rem(tm, 2)
    right, left = lax.rem(anta + 1, ring), lax.rem(anta + ring - 1, ring)
    to_far, to_near, to_pol = {"tm": far}, {"tm": near}, {"antb": 1 - antb}
    sides = ({"anta": right}, {"anta": left})

    barrier = pltpu.get_barrier_semaphore()
    for target in (to_far, to_near, to_pol) + sides:
        pl.semaphore_signal(barrier, inc=1, device_id=target, device_id_type=pl.DeviceIdType.MESH)
    pl.semaphore_wait(barrier, 5)

    started = []

    def send(src, dst, send_sem, recv_sem, target):
        copy = pltpu.make_async_remote_copy(
            src_ref=src, dst_ref=dst, send_sem=send_sem, recv_sem=recv_sem,
            device_id=target, device_id_type=pl.DeviceIdType.MESH)
        copy.start()
        started.append(copy)
        return copy

    times = (tm, far)
    last = ring // 2
    hops, nears = {}, []

    def part(side, hop):
        if hop < last:
            return pl.ds(0, height)
        return pl.ds(side * half, half)

    def pass_on(stream, side, hop, src=None):
        place = lax.rem(anta + (ring - hop + 1 if side == 0 else hop - 1), ring)
        rows = part(side, hop)
        slot = cols.at[times[stream], place, rows]
        src = slot if src is None else src.at[rows]
        hops[stream, side, hop] = send(src, slot, ring_send.at[stream, side, hop - 1],
                                       ring_recv.at[stream, side, hop - 1], sides[side])

    def hand(stream, offset, src=None):
        slot = cols.at[times[stream], lax.rem(anta + offset, ring)]
        nears.append(send(slot if src is None else src, slot, near_send.at[stream, offset],
                          near_recv.at[stream, offset], to_near))

    def arrive(stream, hop):
        for side in range(2):
            hops[stream, side, hop].wait_recv()
            if hop < last:
                pass_on(stream, side, hop + 1)
                hand(stream, ring - hop if side == 0 else hop)
        if hop == last:
            hand(stream, last)

    slot = cols.at[tm, anta]
    first = send(own, slot, far_send.at[0], far_recv.at[0], to_far)
    pol = send(own, other.at[tm], pol_send, pol_recv, to_pol)
    for side in range(2):
        pass_on(0, side, 1, own)
    hand(0, 0, own)
    keep = pltpu.make_async_copy(own, slot, local_sem)
    keep.start()

    first.wait_recv()
    for side in range(2):
        pass_on(1, side, 1)
    hand(1, 0)
    pol.wait_recv()
    second = send(other.at[tm], other.at[tm], far_send.at[1], far_recv.at[1], to_far)
    nears.append(send(other.at[tm], other.at[tm], near_send.at[0, ring], near_recv.at[0, ring], to_near))
    for hop in range(1, last + 1):
        arrive(0, hop)
        if hop == 1:
            second.wait_recv()
            nears.append(send(other.at[far], other.at[far], near_send.at[1, ring],
                              near_recv.at[1, ring], to_near))
        arrive(1, hop)
    for copy in nears:
        copy.wait_recv()
    for copy in started:
        copy.wait_send()
    keep.wait()


def gather(own):
    blocks, ring = lax.axis_size("tm"), lax.axis_size("anta")
    dma = pltpu.SemaphoreType.DMA
    return pl.pallas_call(
        gather_kernel,
        out_shape=[
            jax.ShapeDtypeStruct((blocks, ring) + own.shape, own.dtype),
            jax.ShapeDtypeStruct((blocks,) + own.shape, own.dtype),
        ],
        in_specs=[pl.BlockSpec(memory_space=pltpu.VMEM)],
        out_specs=[pl.BlockSpec(memory_space=pl.ANY)] * 2,
        scratch_shapes=[
            dma, dma((2, 2, ring // 2)), dma((2, 2, ring // 2)), dma((2, ring + 1)), dma((2, ring + 1)),
            dma((2,)), dma((2,)), dma, dma,
        ],
        compiler_params=pltpu.CompilerParams(collective_id=0, has_side_effects=True),
    )(own)


def per_device(samples):
    antennas, width = samples.shape[1:]
    blocks = lax.axis_size("tm")
    lags = LAG_TOTAL // blocks
    own = samples[0].reshape(antennas, LANES, width // LANES).transpose(0, 2, 1).reshape(antennas, width)
    cols, other = gather(own)
    factor = 1.0 / math.sqrt(width * blocks)
    out = correlate(cols, other, lags, factor)
    return out.reshape(lags, -1, antennas, 1, cols.shape[1] * antennas)


def solution(mesh):
    return jax.shard_map(
        per_device,
        mesh=mesh,
        in_specs=(P("antb", "anta", "tm"),),
        out_specs=P("tm", None, "anta", "antb", None),
        check_vma=False,
    )
```

time: 586 us -> 203 us (0.35)
  local copies, waits for them, and re-layouts: 240 us -> 2.33 us
  Pallas kernels: 0 us -> 201 us
  matrix products: 168 us -> 0 us
  waiting for transfers between devices: 134 us -> 0 us
  other arithmetic: 23.9 us -> 0 us
  between operations: 13.1 us -> 0.03 us
    pallas_call x0 -> x2, Pallas kernels: none -> 201 us  [the longest x1 142 us: correlate(): pl.pallas_call(functools.partial(correlate_kernel, factor, stride, lags),...]
    dot_general x8 -> x0, matrix products: 168 us -> none  [one_group(): jnp.einsum('kit,jt->kij', stacked, flat_cols, preferred_element_type=jnp....]
    while x56 -> x0, local copies, waits for them, and re-layouts: 159 us -> none
    all_gather x3 -> x0, waiting for transfers between devices: 133 us -> none  [the longest x1 46.7 us: per_device(): columns = lax.all_gather(col_tiles, 'tm', axis=2, tiled=True)]
    mul x1 -> x0, local copies, waits for them, and re-layouts: 48.4 us -> none  [per_device(): return accumulated_sum * factor]
    mul x1 -> x0, other arithmetic: 23.9 us -> none  [per_device(): return accumulated_sum * factor]
    another operation x8 -> x1, local copies, waits for them, and re-layouts: 22.7 us -> 0.09 us  [per_device(): samples[0].reshape(antennas, LANES, width // LANES).transpose(0, 2, 1)]
    dynamic_slice x9 -> x0, local copies, waits for them, and re-layouts: 7.77 us -> none  [the longest x8 5.07 us: lag_terms(): lax.map(one_group, jnp.arange(lag_count // group_len, dtype=jnp.int32))]
  transfers between devices with their start and end apart: 3 -> 0, of which waited for: 3 -> 0; matrix products, arithmetic and copies ran while one was open for 0% -> 0% of each run, Pallas kernels for 0% -> 0%
where the time goes in v1:
time: 203 us
  Pallas kernels  201 us (99%)
  local copies, waits for them, and re-layouts  2.33 us (1%)
    pallas_call x1, Pallas kernels, correlate(): pl.pallas_call(functools.partial(correlate_kernel, factor, stride, lags),...  142 us
    pallas_call x1, Pallas kernels, gather(): pl.pallas_call(gather_kernel, out_shape=[jax.ShapeDtypeStruct((blocks, ri...  58.8 us

profile of v1, /device:TPU:0, one launch (start us, length us, event | category | flops | bytes accessed | tf_op | source)
XLA Modules:
  0.0 203.2 jit_solution(13483396001448664886)
XLA Ops:
  0.0 1.2 copy.4
  1.2 0.1 reshape_squeeze.3
  1.3 0.1 copy.5
  1.4 0.9 copy.6.own
  2.4 58.8 %shard_map.17 = (bf16[4,4,128,1536]{3,2,1,0:T(8,128)(2,1)}, bf16[4,128,1536]{2,1,0:T(8,128)(2,1)}) custom-call(bf16[128,1536]{1,0:T(8,128)(2,1)} %copy.6.own), custom_call_target="tpu_custom_call" | custom-call | tf_op jit(solution)/shard_map/pallas_call | solution.py:187
  61.1 142.1 %shard_map.18 = f32[64,1024,128]{2,1,0:T(8,128)} custom-call(bf16[4,4,128,1536]{3,2,1,0:T(8,128)(2,1)} %get-tuple-element.7.cols_hbm, bf16[4,128,1536]{2,1,0:T(8,128)(2,1)} %get-tuple-element.8.other_hbm), custom_call_target="tpu_custom_call" | custom-call | tf_op jit(solution)/shard_map/pallas_call | solution.py:80
